TPU v7x, 32 devices: a whole 2x2x4 slice. The times are simulated.
32 devices in a mesh: dp: 16 (over z, x, core), head: 2 (over y).
Axes of the slice: x: 2, y: 2, z: 4, core: 2. Of those that a mesh axis runs over, the one named last changes fastest.
Arguments:
- frames_in: bfloat16 [16, 2, 320, 2560], P('dp', 'head'), may hold values from -6 to 6
- ln1_gain: float32 [1280], replicated, may hold values from 0.25 to 1.75
- ln1_bias: float32 [1280], replicated, may hold values from -3 to 3
- qkv_weight: bfloat16 [1280, 3, 1024], P('dp', None, 'head'), may hold values from -0.1875 to 0.1875
- qv_bias: float32 [2, 1024], P(None, 'head'), may hold values from -3 to 3
- out_weight: bfloat16 [1024, 1280], P(('head', 'dp')), may hold values from -0.1875 to 0.1875
- out_bias: float32 [1280], P('head'), may hold values from -3 to 3
- ln2_gain: float32 [1280], replicated, may hold values from 0.25 to 1.75
- ln2_bias: float32 [1280], replicated, may hold values from -3 to 3
- fc1_weight: bfloat16 [1280, 5120], P('dp', 'head'), may hold values from -0.15625 to 0.15625
- fc1_bias: float32 [5120], P('head'), may hold values from -3 to 3
- fc2_weight: bfloat16 [5120, 1280], P(('head', 'dp')), may hold values from -0.078125 to 0.078125
- fc2_bias: float32 [1280], P('head'), may hold values from -3 to 3
- server_of_clip: int32 [16], replicated, may hold values from 0 to 7
Outputs:
- encoded: bfloat16 [16, 2, 320, 2560], P('dp', 'head')
All inputs are finite; a program needn't handle non-finite values.
Results may differ from a plain program's by a relative error of at most 0.014.
Values may be sent and summed in bfloat16 or wider, within the bound.
A program may use at most 64 MiB of HBM per device.

v0:
```python
import jax
import jax.numpy as jnp
from jax import lax
from jax.sharding import PartitionSpec as P

HDIM = 64


epsilon = 1e-05


def layer_norm(matrix, gain_row, shift_row):
    floats = matrix.astype(jnp.float32)
    center = jnp.mean(floats, axis=-1, keepdims=True)
    spread = jnp.mean(jnp.square(floats - center), axis=-1, keepdims=True)
    return ((floats - center) * lax.rsqrt(spread + epsilon) * gain_row + shift_row).astype(
        jnp.bfloat16
    )


def normalize(residual_in, gain_row, shift_row):
    whole_rows = lax.all_gather(residual_in, "head", axis=1, tiled=True)
    return layer_norm(whole_rows, gain_row, shift_row)


def attend(queries, key_rows, value_rows):

    def single(triple):
        query_head, key_head, value_head = triple
        scores = jnp.dot(query_head, key_head.T, preferred_element_type=jnp.float32)
        maxima = jnp.max(scores, axis=-1, keepdims=True)
        weights = jnp.exp(scores - maxima)
        probability = (weights / jnp.sum(weights, axis=-1, keepdims=True)).astype(jnp.bfloat16)
        return jnp.dot(probability, value_head, preferred_element_type=jnp.float32).astype(
            jnp.bfloat16
        )

    per_head = lax.map(
        single,
        (jnp.swapaxes(queries, 0, 1), jnp.swapaxes(key_rows, 0, 1), jnp.swapaxes(value_rows, 0, 1)),
    )
    return jnp.swapaxes(per_head, 0, 1).reshape(queries.shape[0], -1)


def slot_order(server_list):
    clip_count = server_list.shape[0]
    indices = jnp.arange(clip_count, dtype=jnp.int32)
    earlier = (server_list[None, :] < server_list[:, None]) | (
        server_list[None, :] == server_list[:, None]
    ) & (indices[None, :] < indices[:, None])
    slot_of = jnp.sum(earlier.astype(jnp.int32), axis=1)
    return jnp.sum(jnp.where(slot_of[None, :] == indices[:, None], indices[None, :], 0), axis=1)


def regroup(block_rows, clip_order):
    group_size = lax.axis_size("dp")
    piece_rows = block_rows.reshape(group_size, -1)
    shuffled = lax.all_to_all(piece_rows, "dp", split_axis=0, concat_axis=0, tiled=True)
    picked = jnp.take(shuffled, clip_order, axis=0)
    returned = lax.all_to_all(picked, "dp", split_axis=0, concat_axis=0, tiled=True)
    return returned.reshape(block_rows.shape)


def block_term(operand, weight_rows, row_count, frame_count, local_width):
    blocks = row_count // frame_count
    product = jnp.dot(operand, weight_rows, preferred_element_type=jnp.float32)
    return (
        product.reshape(frame_count, blocks, local_width)
        .transpose(1, 0, 2)
        .reshape(blocks * frame_count, local_width)
    )


def on_device(
    frames_in,
    ln1_gain,
    ln1_bias,
    qkv_weight,
    qv_bias,
    out_weight,
    out_bias,
    ln2_gain,
    ln2_bias,
    fc1_weight,
    fc1_bias,
    fc2_weight,
    fc2_bias,
    server_of_clip,
):
    clip_order = slot_order(server_of_clip)
    group_rows = frames_in.shape[2]
    local_width = frames_in.shape[3] // 4
    frame_count = group_rows * 4
    residual_in = frames_in[0, 0].reshape(frame_count, local_width)
    residual_in = regroup(residual_in, clip_order)
    normed_one = normalize(residual_in, ln1_gain, ln1_bias)
    column_count = qkv_weight.shape[2]
    weight_piece = lax.all_gather(qkv_weight, "dp", axis=0, tiled=True)
    operand = normed_one
    projected = jnp.dot(
        operand, weight_piece.reshape(weight_piece.shape[0], -1), preferred_element_type=jnp.float32
    ).reshape(frame_count, 3, column_count)
    queries = (
        ((projected[:, 0] + qv_bias[0]) * HDIM ** (-0.5))
        .astype(jnp.bfloat16)
        .reshape(frame_count, -1, HDIM)
    )
    key_rows = projected[:, 1].astype(jnp.bfloat16).reshape(frame_count, -1, HDIM)
    value_rows = (projected[:, 2] + qv_bias[1]).astype(jnp.bfloat16).reshape(frame_count, -1, HDIM)
    context = attend(queries, key_rows, value_rows)
    output_rows = lax.all_gather(out_weight, "dp", axis=0, tiled=True)
    carried = residual_in.astype(jnp.float32) + out_bias
    attended = (
        carried
        + lax.psum_scatter(
            block_term(
                context, output_rows, frame_count * lax.axis_size("head"), frame_count, local_width
            ).astype(jnp.bfloat16),
            "head",
            scatter_dimension=0,
            tiled=True,
        ).astype(jnp.float32)
    ).astype(jnp.bfloat16)
    normed_two = normalize(attended, ln2_gain, ln2_bias)
    operand = normed_two
    hidden_sums = jnp.dot(
        operand,
        lax.all_gather(fc1_weight, "dp", axis=0, tiled=True),
        preferred_element_type=jnp.float32,
    )
    hidden = jax.nn.gelu(hidden_sums + fc1_bias, approximate=False).astype(jnp.bfloat16)
    down_rows = lax.all_gather(fc2_weight, "dp", axis=0, tiled=True)
    kept = attended.astype(jnp.float32) + fc2_bias
    layer_out = (
        kept
        + lax.psum_scatter(
            block_term(
                hidden, down_rows, frame_count * lax.axis_size("head"), frame_count, local_width
            ).astype(jnp.bfloat16),
            "head",
            scatter_dimension=0,
            tiled=True,
        ).astype(jnp.float32)
    ).astype(jnp.bfloat16)
    return layer_out.reshape(1, 1, group_rows, 4 * local_width)


def solution(mesh):
    placed = (
        P("dp", "head", None, None),
        P(),
        P(),
        P("dp", None, "head"),
        P(None, "head"),
        P(("head", "dp"), None),
        P("head"),
        P(),
        P(),
        P("dp", "head"),
        P("head"),
        P(("head", "dp"), None),
        P("head"),
        P(),
    )
    return jax.shard_map(
        on_device,
        mesh=mesh,
        in_specs=placed,
        out_specs=P("dp", "head", None, None),
        check_vma=False,
    )
```

profile of v0, /device:TPU:0, one launch (start us, length us, event | category | flops | bytes accessed | tf_op | source)
XLA Modules:
  0.0 602.3 jit_solution(14963864365665853193)
XLA Ops:
  7.3 4.3 all_to_all.16
  12.1 11.7 %reduce.9 = bf16[16,51200]{1,0:T(8,128)(2,1)} reduce(bf16[16,1,51200]{2,1,0:T(2,128)(2,1)S(1)} %all_to_all.16, bf16[]{:T(256)} %broadcast.140), dimensions={1}, to_apply=%all_to_all.16.reduce_sub_computation | reduce | bytes 3276802 | tf_op jit(solution)/shard_map/all_to_all | solution.py:58
  23.7 3.4 reshape.149
  27.1 7.4 %all-to-all-start = ((bf16[16,2,25600]{2,1,0:T(2,128)(2,1)}), bf16[16,2,25600]{2,1,0:T(2,128)(2,1)S(1)}, u32[]{:S(2)}, u32[]{:S(2)}) async-start(bf16[16,2,25600]{2,1,0:T(2,128)(2,1)} %reshape.149), calls=%async_computation | async-start | bytes 3276800 | tf_op jit(solution)/shard_map/all_to_all | solution.py:58
  36.0 36.7 %all-to-all-done = bf16[16,2,25600]{2,1,0:T(2,128)(2,1)S(1)} async-done(((bf16[16,2,25600]{2,1,0:T(2,128)(2,1)}), bf16[16,2,25600]{2,1,0:T(2,128)(2,1)S(1)}, u32[]{:S(2)}, u32[]{:S(2)}) %all-to-all-start) | async-done | bytes 1638432 | tf_op jit(solution)/shard_map/all_to_all | solution.py:58
  72.7 6.2 %reshape.150 = bf16[16,1,51200]{2,1,0:T(2,128)(2,1)} reshape(bf16[16,2,25600]{2,1,0:T(2,128)(2,1)S(1)} %all-to-all-done) | data formatting | bytes 3276800
  78.8 2.9 copy.58
  81.7 2.8 gather_fusion
  89.4 58.1 %all_to_all.19 = bf16[16,2,25600]{2,1,0:T(2,128)(2,1)} all-to-all(bf16[16,2,25600]{2,1,0:T(2,128)(2,1)S(1)} %reshape.151), channel_id=1, replica_groups=mesh['dp'=16,'head'=2] {'dp'}, dimensions={0} | all-to-all | bytes 3276800 | tf_op jit(solution)/shard_map/all_to_all | solution.py:60
  147.4 8.0 %reshape.152 = bf16[16,1,51200]{2,1,0:T(2,128)(2,1)S(1)} reshape(bf16[16,2,25600]{2,1,0:T(2,128)(2,1)} %all_to_all.19) | data formatting | bytes 3276800
  155.4 11.1 %reduce = bf16[16,51200]{1,0:T(8,128)(2,1)} reduce(bf16[16,1,51200]{2,1,0:T(2,128)(2,1)S(1)} %reshape.152, bf16[]{:T(256)} %constant.106), dimensions={1}, to_apply=%all_to_all.15.reduce_sub_computation | reduce | bytes 3276802 | tf_op jit(solution)/shard_map/all_to_all | solution.py:60
  166.6 2.8 reshape.122
  169.8 2.5 copy.51
  172.3 6.4 %copy.47 = bf16[1280,3,512]{0,2,1:T(8,128)(2,1)} copy(bf16[1280,3,512]{2,0,1:T(8,128)(2,1)} %all-gather.9.cloned.1.call-done) | data formatting | bytes 7864320 | tf_op jit(solution)/shard_map/all_gather | solution.py:98
  178.7 36.6 %all-gather.7.cloned.1.call-done = bf16[1280,1280]{1,0:T(8,128)(2,1)} async-done(((bf16[1280,640]{1,0:T(8,128)(2,1)}), bf16[1280,1280]{1,0:T(8,128)(2,1)}) %all-gather.7.cloned.1.call-update) | async-done | bytes 3276816 | tf_op jit(solution)/shard_map/all_gather | solution.py:22
  215.3 2.6 convert_reduce_fusion.1
  217.9 2.9 fusion.32
  220.8 7.8 %fusion.36 = f32[1280,3,512]{0,2,1:T(8,128)S(1)} fusion(bf16[1280,3,512]{0,2,1:T(8,128)(2,1)} %copy.47, bf16[1280,1280]{1,0:T(8,128)(2,1)S(1)} %copy-done.2, f32[1280]{0:T(1024)S(1)} %copy-done.8, f32[1280]{0:T(1024)S(1)} %copy-done.9, f32[1280]{0:T(1024)S(1)} %add_rsqrt_fusion.1, f32[1280]{0:T(1024)S(1)} %broadcast_multiply_fusion.1), kind=kOutput, calls=%fused_computation.57 | convolution fusion | flops 5042995200 | bytes 15093760 | tf_op jit(solution)/shard_map/dot_general | solution.py:100
  231.7 5.0 copy.48
  236.7 3.7 copy.50
  240.4 3.8 copy.49
  244.2 6.8 %fusion.54 = (bf16[8,1280,64]{2,1,0:T(8,128)(2,1)S(1)}, bf16[8,1280,64]{2,1,0:T(8,128)(2,1)}) fusion(f32[1280,8,64]{2,0,1:T(8,128)} %copy.48, f32[8,64]{1,0:T(8,128)S(1)} %add.113, f32[1280,8,64]{2,0,1:T(8,128)} %copy.50, f32[8,64]{1,0:T(8,128)S(1)} %add.116), kind=kLoop, calls=%fused_computation.70 | loop fusion | flops 3276800 | bytes 7868416 | tf_op jit(solution)/shard_map/transpose | solution.py:40
  250.9 47.2 %while.10 = (s32[]{:T(128)}, bf16[8,1280,64]{1,2,0:T(8,128)(2,1)}, bf16[8,1280,64]{2,1,0:T(8,128)(2,1)S(1)}, bf16[8,1280,64]{2,1,0:T(8,128)(2,1)}, bf16[8,1280,64]{2,1,0:T(8,128)(2,1)}, /*index=5*/s32[]{:T(128)}) while((s32[]{:T(128)}, bf16[8,1280,64]{1,2,0:T(8,128)(2,1)}, bf16[8,1280,64]{2,1,0:T(8,128)(2,1)S(1)}, ...), condition=%wide.region_7.8_spmd, body=%wide.region_4.7_spmd.sunk | while | flops 429340160 | bytes 20835396 | solution.py:38
  251.1 2.0 fusion.108
  254.1 2.9 fusion.110
  257.0 2.0 fusion.108
  260.0 2.9 fusion.110
  265.9 2.9 fusion.110
  268.8 2.0 fusion.108
  271.7 2.9 fusion.110
  274.6 2.0 fusion.108
  277.6 2.9 fusion.110
  280.5 2.0 fusion.108
  283.5 2.9 fusion.110
  289.4 2.9 fusion.110
  295.2 2.9 fusion.110
  298.2 5.4 convolution_convert_fusion.1
  303.7 44.9 %reduce-scatter.3.cloned.1.call-done = bf16[1280,640]{1,0:T(8,128)(2,1)} async-done(((bf16[2560,640]{1,0:T(8,128)(2,1)}), bf16[1280,640]{1,0:T(8,128)(2,1)}) %reduce-scatter.3.cloned.1.call-update) | async-done | bytes 1638416 | tf_op jit(solution)/shard_map/reduce_scatter | solution.py:115
  348.6 3.1 add_convert_fusion.2
  353.1 45.2 %all-gather.13.cloned.1.call-done = bf16[1280,1280]{1,0:T(8,128)(2,1)} async-done(((bf16[1280,640]{1,0:T(8,128)(2,1)}), bf16[1280,1280]{1,0:T(8,128)(2,1)}) %all-gather.13.cloned.1.call-update) | async-done | bytes 3276816 | tf_op jit(solution)/shard_map/all_gather | solution.py:22
  398.3 2.6 convert_reduce_fusion
  400.9 2.9 fusion.28
  403.8 59.5 %all-gather.15.cloned.1.call-done = bf16[1280,2560]{1,0:T(8,128)(2,1)} async-done(((bf16[80,2560]{1,0:T(8,128)(2,1)}), bf16[1280,2560]{1,0:T(8,128)(2,1)}) %all-gather.15.cloned.1.call-update) | async-done | bytes 6553616 | tf_op jit(solution)/shard_map/all_gather | solution.py:128
  463.3 40.8 %fusion.16.clone.4 = bf16[1280,2560]{1,0:T(8,128)(2,1)} fusion(f32[2560]{0:T(1024)S(1)} %copy-done.7, bf16[1280,2560]{1,0:T(8,128)(2,1)} %all-gather.15.cloned.1.call-done, bf16[1280,1280]{1,0:T(8,128)(2,1)S(1)} %copy-done.3, f32[1280]{0:T(1024)S(1)} %copy-done.10, f32[1280]{0:T(1024)S(1)} %copy-done.11, f32[1280]{0:T(1024)S(1)} %add_rsqrt_fusion, ...), kind=kOutput, calls=%fused_computation.21.clone.clone.clone.1 | convolution fusion | flops 8614707200 | bytes 16414720 | tf_op jit(solution)/shard_map/dot_general | solution.py:126
  504.1 23.1 %all-gather.17.cloned.1.call-done = bf16[2560,1280]{1,0:T(8,128)(2,1)} async-done(((bf16[160,1280]{1,0:T(8,128)(2,1)}), bf16[2560,1280]{1,0:T(8,128)(2,1)}) %all-gather.17.cloned.1.call-update) | async-done | bytes 6553616 | tf_op jit(solution)/shard_map/all_gather | solution.py:132
  527.2 14.3 %convolution_convert_fusion = bf16[1280,1280]{0,1:T(8,128)(2,1)} fusion(bf16[2560,1280]{1,0:T(8,128)(2,1)} %all-gather.17.cloned.1.call-done, bf16[1280,2560]{1,0:T(8,128)(2,1)} %fusion.16.clone.4), kind=kOutput, calls=%fused_computation.45 | convolution fusion | flops 8390246400 | bytes 16384000 | tf_op jit(solution)/shard_map/dot_general | solution.py:66
  541.5 5.8 copy.53
  547.4 43.8 %reduce-scatter.5.cloned.1.call-done = bf16[1280,640]{1,0:T(8,128)(2,1)} async-done(((bf16[2560,640]{1,0:T(8,128)(2,1)}), bf16[1280,640]{1,0:T(8,128)(2,1)}) %reduce-scatter.5.cloned.1.call-update) | async-done | bytes 1638416 | tf_op jit(solution)/shard_map/reduce_scatter | solution.py:136
  (76 shorter events, 30.0 us)
Async XLA Ops:
  6.5 163.3 %all-gather.11.cloned.1.call-start = ((), (), s32[]{:S(2)}) async-start(), calls=%async_computation.6 | async-start | bytes 1392640 | tf_op jit(solution)/shard_map/all_gather | solution.py:111
  11.6 24.1 %copy-start.12 = (s32[16]{0:T(128)S(1)}, s32[16]{0:T(128)}, u32[]{:S(2)}) copy-start(s32[16]{0:T(128)} %param.29) | copy-start | bytes 196
  27.1 45.6 %all-to-all-start = ((bf16[16,2,25600]{2,1,0:T(2,128)(2,1)}), bf16[16,2,25600]{2,1,0:T(2,128)(2,1)S(1)}, u32[]{:S(2)}, u32[]{:S(2)}) async-start(bf16[16,2,25600]{2,1,0:T(2,128)(2,1)} %reshape.149), calls=%async_computation | async-start | bytes 3276800 | tf_op jit(solution)/shard_map/all_to_all | solution.py:58
  34.5 137.8 %all-gather.9.cloned.1.call-start = ((), (), s32[]{:S(2)}) async-start(), calls=%async_computation.5 | async-start | bytes 4177920 | tf_op jit(solution)/shard_map/all_gather | solution.py:98
  35.3 180.0 %all-gather.7.cloned.1.call-start = ((), (), s32[]{:S(2)}) async-start(), calls=%async_computation.4 | async-start | bytes 4915200 | tf_op jit(solution)/shard_map/all_gather | solution.py:22
  147.4 22.2 %copy-start.4 = (f32[2,512]{1,0:T(2,128)S(1)}, f32[2,512]{1,0:T(2,128)}, u32[]{:S(2)}) copy-start(f32[2,512]{1,0:T(2,128)} %param.20) | copy-start | bytes 12292
  169.4 179.2 %reduce-scatter.3.cloned.1.call-start = ((), (), s32[]{:S(2)}) async-start(), calls=%async_computation.7 | async-start | bytes 4915200 | tf_op jit(solution)/shard_map/reduce_scatter | solution.py:115
  172.3 48.5 %copy-start.8 = (f32[1280]{0:T(1024)S(1)}, f32[1280]{0:T(1024)}, u32[]{:S(2)}) copy-start(f32[1280]{0:T(1024)} %param.18) | copy-start | bytes 15364
  172.3 48.6 %copy-start.9 = (f32[1280]{0:T(1024)S(1)}, f32[1280]{0:T(1024)}, u32[]{:S(2)}) copy-start(f32[1280]{0:T(1024)} %param.17) | copy-start | bytes 15364
  215.3 5.5 copy-start.2
  298.2 50.5 %copy-start = (bf16[1280,640]{1,0:T(8,128)(2,1)S(1)}, bf16[1280,640]{1,0:T(8,128)(2,1)}, u32[]{:S(2)}) copy-start(bf16[1280,640]{1,0:T(8,128)(2,1)} %reshape.122) | copy-start | bytes 4915204
  298.2 50.5 %copy-start.5 = (f32[640]{0:T(1024)S(1)}, f32[640]{0:T(1024)}, u32[]{:S(2)}) copy-start(f32[640]{0:T(1024)} %param.22) | copy-start | bytes 7684
  303.6 159.7 %copy-start.7 = (f32[2560]{0:T(1024)S(1)}, f32[2560]{0:T(1024)}, u32[]{:S(2)}) copy-start(f32[2560]{0:T(1024)} %param.26) | copy-start | bytes 30724
  303.6 159.7 %copy-start.10 = (f32[1280]{0:T(1024)S(1)}, f32[1280]{0:T(1024)}, u32[]{:S(2)}) copy-start(f32[1280]{0:T(1024)} %param.24) | copy-start | bytes 15364
  303.6 159.7 %copy-start.11 = (f32[1280]{0:T(1024)S(1)}, f32[1280]{0:T(1024)}, u32[]{:S(2)}) copy-start(f32[1280]{0:T(1024)} %param.23) | copy-start | bytes 15364
  303.7 94.6 %all-gather.13.cloned.1.call-start = ((), (), s32[]{:S(2)}) async-start(), calls=%async_computation.8 | async-start | bytes 4915200 | tf_op jit(solution)/shard_map/all_gather | solution.py:22
  351.7 111.6 %all-gather.15.cloned.1.call-start = ((), (), s32[]{:S(2)}) async-start(), calls=%async_computation.9 | async-start | bytes 6963200 | tf_op jit(solution)/shard_map/all_gather | solution.py:128
  352.3 174.9 %all-gather.17.cloned.1.call-start = ((), (), s32[]{:S(2)}) async-start(), calls=%async_computation.10 | async-start | bytes 6963200 | tf_op jit(solution)/shard_map/all_gather | solution.py:132
  353.1 238.1 %reduce-scatter.5.cloned.1.call-start = ((), (), s32[]{:S(2)}) async-start(), calls=%async_computation.11 | async-start | bytes 4915200 | tf_op jit(solution)/shard_map/reduce_scatter | solution.py:136
  398.3 65.0 %copy-start.3 = (bf16[1280,1280]{1,0:T(8,128)(2,1)S(1)}, bf16[1280,1280]{1,0:T(8,128)(2,1)}, u32[]{:S(2)}) copy-start(bf16[1280,1280]{1,0:T(8,128)(2,1)} %all-gather.13.cloned.1.call-done) | copy-start | bytes 9830404
  541.5 49.6 %copy-start.1 = (bf16[1280,640]{1,0:T(8,128)(2,1)S(1)}, bf16[1280,640]{1,0:T(8,128)(2,1)}, u32[]{:S(2)}) copy-start(bf16[1280,640]{1,0:T(8,128)(2,1)} %add_convert_fusion.2) | copy-start | bytes 4915204
  541.5 49.6 %copy-start.6 = (f32[640]{0:T(1024)S(1)}, f32[640]{0:T(1024)}, u32[]{:S(2)}) copy-start(f32[640]{0:T(1024)} %param.28) | copy-start | bytes 7684
Sparse Core Ops, SparseCore 0:
  9.6 48.2 all-gather.10
  60.2 57.7 all-gather.8
  169.5 45.7 all-gather.6
  303.7 44.8 reduce-scatter.2
  351.9 46.3 all-gather.12
  400.4 62.8 all-gather.14
  465.6 61.5 all-gather.16
  547.5 43.6 reduce-scatter.4
where the time goes:
time: 612 us; the launch traced here: 602 us
  waiting for transfers between devices  292 us (48%)
  matrix products  108 us (18%)
  local copies, waits for them, and re-layouts  64.6 us (11%)
  blocking collectives  58.1 us (9%)
  other arithmetic  57.1 us (9%)
  between operations  14.2 us (2%)
  starting transfers between devices  8.18 us (1%)
    all_gather x2, waiting for transfers between devices, normalize(): whole_rows = lax.all_gather(residual_in, 'head', axis=1, tiled=True)  81.7 us
    all_gather x1, waiting for transfers between devices, on_device(): lax.all_gather(fc1_weight, 'dp', axis=0, tiled=True)  59.5 us
    all_to_all x1, blocking collectives, regroup(): lax.all_to_all(picked, 'dp', split_axis=0, concat_axis=0, tiled=True)  58.1 us
    reduce_scatter x1, waiting for transfers between devices, on_device(): lax.psum_scatter(block_term(context, output_rows, frame_count * lax.axis_...  44.9 us
    reduce_scatter x1, waiting for transfers between devices, on_device(): lax.psum_scatter(block_term(hidden, down_rows, frame_count * lax.axis_siz...  43.8 us
    dot_general x1, matrix products, on_device(): jnp.dot(operand, lax.all_gather(fc1_weight, 'dp', axis=0, tiled=True), pr...  40.8 us
    all_to_all x1, waiting for transfers between devices, regroup(): lax.all_to_all(piece_rows, 'dp', split_axis=0, concat_axis=0, tiled=True)  36.7 us
    dot_general x8, matrix products, single(): jnp.dot(probability, value_head, preferred_element_type=jnp.float32)  23.2 us
  transfers between devices with their start and end apart: 9, of which 7 were waited for; matrix products, arithmetic and copies ran while one was open for 18% of the time, Pallas kernels for 0%

commit v1 on v0

--- a/solution.py
+++ b/solution.py
@@ -1,6 +1,10 @@
+import functools
+
 import jax
 import jax.numpy as jnp
 from jax import lax
+from jax.experimental import pallas as pl
+from jax.experimental.pallas import tpu as pltpu
 from jax.sharding import PartitionSpec as P
 
 HDIM = 64
@@ -145,6 +149,396 @@
     return layer_out.reshape(1, 1, group_rows, 4 * local_width)
 
 
+MESH = pl.DeviceIdType.MESH
+VMEM = pltpu.MemorySpace.VMEM
+LIMIT = 60000000
+
+
+def at_rows(index, rows):
+    return pl.ds(pl.multiple_of(index * rows, rows), rows)
+
+
+def greet(peers):
+    barrier = pltpu.get_barrier_semaphore()
+    for peer in peers:
+        pl.semaphore_signal(barrier, inc=1, device_id=peer, device_id_type=MESH)
+    pl.semaphore_wait(barrier, len(peers))
+
+
+def regroup_kernel(dp, heads, order_ref, x_ref, o_ref, first, second, s1, r1, s2, r2, s3, r3):
+    me, h = lax.axis_index("dp"), lax.axis_index("head")
+    rows, width = first.shape[1:]
+    row_blocks = x_ref.shape[0] // rows
+    greet(
+        [(lax.rem(me + k, dp), h) for k in range(1, dp)]
+        + [(me, lax.rem(h + j, heads)) for j in range(1, heads)]
+    )
+
+    def taken(c):
+        return x_ref.at[
+            at_rows(lax.rem(c, row_blocks), rows), at_rows(lax.div(c, row_blocks), width)
+        ]
+
+    def placed(c):
+        return o_ref.at[at_rows(c, rows), at_rows(h, width)]
+
+    def one(k):
+        other = lax.rem(me + k, dp)
+        return pltpu.make_async_remote_copy(
+            taken(other), first.at[me], s1.at[k], r1.at[k], (other, h), MESH
+        )
+
+    def two(k):
+        other = lax.rem(me + k, dp)
+        return pltpu.make_async_remote_copy(
+            second.at[other], placed(me), s2.at[k], r2.at[k], (other, h), MESH
+        )
+
+    def three(k, j):
+        ref = placed(lax.rem(me - k + dp, dp))
+        return pltpu.make_async_remote_copy(
+            ref, ref, s3.at[j - 1, k], r3.at[j - 1, k], (me, lax.rem(h + j, heads)), MESH
+        )
+
+    def loop(start, body):
+        def step(k, carry):
+            body(k)
+            return carry
+
+        lax.fori_loop(start, dp, step, 0)
+
+    loop(1, lambda k: one(k).start())
+    own = pltpu.make_async_copy(taken(me), first.at[me], r1.at[0])
+    own.start()
+    own.wait()
+    loop(1, lambda k: one(k).wait_recv())
+
+    def pick(k):
+        other = lax.rem(me + k, dp)
+        second[other] = first[order_ref[other]]
+
+    loop(0, pick)
+    loop(1, lambda k: two(k).start())
+    own = pltpu.make_async_copy(second.at[me], placed(me), r2.at[0])
+    own.start()
+    own.wait()
+    for j in range(1, heads):
+        three(0, j).start()
+
+    def forward(k):
+        two(k).wait_recv()
+        for j in range(1, heads):
+            three(k, j).start()
+
+    loop(1, forward)
+
+    def finish(k):
+        for j in range(1, heads):
+            three(k, j).wait()
+
+    loop(0, finish)
+    loop(1, lambda k: one(k).wait_send())
+    loop(1, lambda k: two(k).wait_send())
+
+
+def regroup_gather(frames, clip_order, dp, heads, width):
+    groups = frames.shape[0]
+    rows = groups * 4 // dp
+    sems = [pltpu.SemaphoreType.DMA((dp,))] * 4 + [pltpu.SemaphoreType.DMA((heads - 1, dp))] * 2
+    return pl.pallas_call(
+        functools.partial(regroup_kernel, dp, heads),
+        out_shape=jax.ShapeDtypeStruct((groups * 4, heads * width), frames.dtype),
+        in_specs=[
+            pl.BlockSpec(memory_space=pltpu.MemorySpace.SMEM),
+            pl.BlockSpec(memory_space=VMEM),
+        ],
+        out_specs=pl.BlockSpec(memory_space=VMEM),
+        scratch_shapes=[pltpu.VMEM((dp, rows, width), frames.dtype)] * 2 + sems,
+        compiler_params=pltpu.CompilerParams(
+            collective_id=0, has_side_effects=True, vmem_limit_bytes=24000000
+        ),
+        cost_estimate=pl.CostEstimate(flops=0, bytes_accessed=200000000, transcendentals=0),
+        name="regroup",
+    )(clip_order, frames)
+
+
+def norm_rows(floats, gain, shift):
+    center = jnp.mean(floats, axis=-1, keepdims=True)
+    moved = floats - center
+    spread = jnp.mean(jnp.square(moved), axis=-1, keepdims=True)
+    return (moved * lax.rsqrt(spread + epsilon) * gain + shift).astype(jnp.bfloat16)
+
+
+def project_kernel(x_ref, gain_ref, shift_ref, w_ref, b_ref, q_ref, k_ref, v_ref):
+    n = q_ref.shape[1]
+    normed = norm_rows(x_ref[...].astype(jnp.float32), gain_ref[...], shift_ref[...])
+
+    def part(i):
+        return jnp.dot(normed, w_ref[:, i * n : (i + 1) * n], preferred_element_type=jnp.float32)
+
+    q_ref[...] = ((part(0) + b_ref[0:1]) * HDIM ** (-0.5)).astype(jnp.bfloat16)
+    k_ref[...] = part(1).astype(jnp.bfloat16)
+    v_ref[...] = (part(2) + b_ref[1:2]).astype(jnp.bfloat16)
+
+
+def project(x, gain, shift, weight, bias, block):
+    rows, depth = x.shape
+    n = weight.shape[1] // 3
+    whole = pl.BlockSpec(memory_space=VMEM)
+    spec = pl.BlockSpec((block, n), lambda i: (i, 0))
+    return pl.pallas_call(
+        project_kernel,
+        grid=(rows // block,),
+        out_shape=[jax.ShapeDtypeStruct((rows, n), jnp.bfloat16)] * 3,
+        in_specs=[pl.BlockSpec((block, depth), lambda i: (i, 0)), whole, whole, whole, whole],
+        out_specs=[spec] * 3,
+        compiler_params=pltpu.CompilerParams(vmem_limit_bytes=32000000),
+        cost_estimate=pl.CostEstimate(
+            flops=2 * rows * depth * 3 * n, bytes_accessed=12000000, transcendentals=0
+        ),
+        name="project",
+    )(x, gain, shift, weight, bias)
+
+
+def attend_kernel(heads, block, q_ref, k_ref, v_ref, o_ref, send, recv):
+    me, h = lax.axis_index("dp"), lax.axis_index("head")
+    frames, columns = q_ref.shape
+    pair = 2 * HDIM
+    pairs = columns // pair
+    greet([(me, lax.rem(h + j, heads)) for j in range(1, heads)])
+    lane = lax.broadcasted_iota(jnp.int32, (1, pair), 1)
+    low_f = jnp.where(lane < HDIM, 1.0, 0.0)
+    low, high = low_f.astype(jnp.bfloat16), (1.0 - low_f).astype(jnp.bfloat16)
+
+    def copy(p, j):
+        ref = o_ref.at[:, at_rows(h * pairs + p, pair)]
+        return pltpu.make_async_remote_copy(
+            ref, ref, send.at[j - 1, p], recv.at[j - 1, p], (me, lax.rem(h + j, heads)), MESH
+        )
+
+    def each_pair(p, carry):
+        cols = at_rows(p, pair)
+        keys, values = k_ref[:, cols], v_ref[:, cols]
+        value_low, value_high = values * low + high, values * high + low
+
+        def head(query, value):
+            scores = lax.dot_general(
+                query, keys, (((1,), (1,)), ((), ())), preferred_element_type=jnp.float32
+            )
+            top = jnp.max(scores, axis=-1, keepdims=True)
+            weights = jnp.exp(scores - top).astype(jnp.bfloat16)
+            return jnp.dot(weights, value, preferred_element_type=jnp.float32)
+
+        def each_block(b, inner):
+            rows = at_rows(b, block)
+            query = q_ref[rows, cols]
+            first = head(query * low, value_low)
+            second = head(query * high, value_high)
+            top = first * low_f + second * (1.0 - low_f)
+            total = pltpu.roll(first * (1.0 - low_f) + second * low_f, HDIM, 1)
+            o_ref[rows, at_rows(h * pairs + p, pair)] = (top / total).astype(jnp.bfloat16)
+            return inner
+
+        lax.fori_loop(0, frames // block, each_block, 0)
+        for j in range(1, heads):
+            copy(p, j).start()
+        return carry
+
+    lax.fori_loop(0, pairs, each_pair, 0)
+
+    def finish(p, carry):
+        for j in range(1, heads):
+            copy(p, j).wait()
+        return carry
+
+    lax.fori_loop(0, pairs, finish, 0)
+
+
+def attend_gather(q, k, v, heads, block):
+    frames, columns = q.shape
+    pairs = columns // (2 * HDIM)
+    whole = pl.BlockSpec(memory_space=VMEM)
+    return pl.pallas_call(
+        functools.partial(attend_kernel, heads, block),
+        out_shape=jax.ShapeDtypeStruct((frames, heads * columns), q.dtype),
+        in_specs=[whole] * 3,
+        out_specs=whole,
+        scratch_shapes=[pltpu.SemaphoreType.DMA((heads - 1, pairs))] * 2,
+        compiler_params=pltpu.CompilerParams(
+            collective_id=1, has_side_effects=True, vmem_limit_bytes=32000000
+        ),
+        cost_estimate=pl.CostEstimate(
+            flops=20000000000, bytes_accessed=6000000, transcendentals=13000000
+        ),
+        name="attend",
+    )(q, k, v)
+
+
+def output_kernel(x_ref, c_ref, w_ref, bias_ref, gain_ref, shift_ref, a_ref, n_ref):
+    product = jnp.dot(c_ref[...], w_ref[...], preferred_element_type=jnp.float32)
+    attended = (x_ref[...].astype(jnp.float32) + bias_ref[...] + product).astype(jnp.bfloat16)
+    a_ref[...] = attended
+    n_ref[...] = norm_rows(attended.astype(jnp.float32), gain_ref[...], shift_ref[...])
+
+
+def output_norm(x, context, weight, bias, gain, shift, block):
+    rows, depth = x.shape
+    whole = pl.BlockSpec(memory_space=VMEM)
+    spec = pl.BlockSpec((block, depth), lambda i: (i, 0))
+    return pl.pallas_call(
+        output_kernel,
+        grid=(rows // block,),
+        out_shape=[jax.ShapeDtypeStruct((rows, depth), jnp.bfloat16)] * 2,
+        in_specs=[
+            spec,
+            pl.BlockSpec((block, context.shape[1]), lambda i: (i, 0)),
+            whole,
+            whole,
+            whole,
+            whole,
+        ],
+        out_specs=[spec] * 2,
+        compiler_params=pltpu.CompilerParams(vmem_limit_bytes=32000000),
+        cost_estimate=pl.CostEstimate(
+            flops=2 * rows * depth * context.shape[1], bytes_accessed=14000000, transcendentals=0
+        ),
+        name="output",
+    )(x, context, weight, bias, gain, shift)
+
+
+def feed_kernel(
+    heads, tile, n_ref, a_ref, w1_ref, b1_ref, w2_ref, b2_ref, o_ref, hidden, kept, out, got, s, r
+):
+    me, h = lax.axis_index("dp"), lax.axis_index("head")
+    blocks, rows, width = kept.shape
+    greet([(me, lax.rem(h + j, heads)) for j in range(1, heads)])
+
+    def copy(b, j):
+        return pltpu.make_async_remote_copy(
+            out.at[j - 1, b],
+            got.at[j - 1, b],
+            s.at[j - 1, b],
+            r.at[j - 1, b],
+            (me, lax.rem(h + j, heads)),
+            MESH,
+        )
+
+    def share(target):
+        return jnp.dot(
+            hidden[...], w2_ref[:, at_rows(target, width)], preferred_element_type=jnp.float32
+        )
+
+    def each_block(b, carry):
+        at = at_rows(b, rows)
+
+        def each_tile(t, inner):
+            cols = at_rows(t, tile)
+            sums = jnp.dot(n_ref[at, :], w1_ref[:, cols], preferred_element_type=jnp.float32)
+            sums = sums + b1_ref[:, cols]
+            hidden[:, cols] = (0.5 * sums * (1.0 + lax.erf(sums * 0.7071067811865476))).astype(
+                jnp.bfloat16
+            )
+            return inner
+
+        lax.fori_loop(0, w1_ref.shape[1] // tile, each_tile, 0)
+        for j in range(1, heads):
+            out[j - 1, b] = share(lax.rem(h + j, heads)).astype(jnp.bfloat16)
+            copy(b, j).start()
+        kept[b] = a_ref[at, at_rows(h, width)].astype(jnp.float32) + b2_ref[...] + share(h)
+        return carry
+
+    lax.fori_loop(0, blocks, each_block, 0)
+    for b in range(blocks):
+        total = kept[b]
+        for j in range(1, heads):
+            copy(b, j).wait()
+            total = total + got[j - 1, b].astype(jnp.float32)
+        o_ref[:, b * width : (b + 1) * width] = total.astype(jnp.bfloat16)
+
+
+def feed_forward(normed, attended, w1, b1, w2, b2, heads, tile):
+    frames, depth = normed.shape
+    width = depth // heads
+    rows = frames // 4
+    whole = pl.BlockSpec(memory_space=VMEM)
+    return pl.pallas_call(
+        functools.partial(feed_kernel, heads, tile),
+        out_shape=jax.ShapeDtypeStruct((rows, 4 * width), jnp.bfloat16),
+        in_specs=[whole] * 6,
+        out_specs=whole,
+        scratch_shapes=[
+            pltpu.VMEM((rows, w1.shape[1]), jnp.bfloat16),
+            pltpu.VMEM((4, rows, width), jnp.float32),
+            pltpu.VMEM((heads - 1, 4, rows, width), jnp.bfloat16),
+            pltpu.VMEM((heads - 1, 4, rows, width), jnp.bfloat16),
+            pltpu.SemaphoreType.DMA((heads - 1, 4)),
+            pltpu.SemaphoreType.DMA((heads - 1, 4)),
+        ],
+        compiler_params=pltpu.CompilerParams(
+            collective_id=2, has_side_effects=True, vmem_limit_bytes=LIMIT
+        ),
+        cost_estimate=pl.CostEstimate(
+            flops=4 * frames * depth * w1.shape[1], bytes_accessed=40000000, transcendentals=0
+        ),
+        name="feed",
+    )(normed, attended, w1, b1, w2, b2)
+
+
+def on_device_aligned(
+    frames_in,
+    ln1_gain,
+    ln1_bias,
+    qkv_weight,
+    qv_bias,
+    out_weight,
+    out_bias,
+    ln2_gain,
+    ln2_bias,
+    fc1_weight,
+    fc1_bias,
+    fc2_weight,
+    fc2_bias,
+    server_of_clip,
+):
+    dp, heads = lax.axis_size("dp"), lax.axis_size("head")
+    width = frames_in.shape[3] // 4
+    block = frames_in.shape[2] * 4 // 5
+    whole_bias = lax.all_gather(out_bias, "head", axis=0, tiled=True)
+    w_qkv = lax.all_gather(
+        qkv_weight.reshape(qkv_weight.shape[0], -1), "dp", axis=0, tiled=True
+    )
+    w_out = lax.all_gather(out_weight, ("head", "dp"), axis=0, tiled=True)
+    w_up = lax.all_gather(fc1_weight, "dp", axis=0, tiled=True)
+    w_down = lax.all_gather(fc2_weight, "dp", axis=0, tiled=True)
+    residual = regroup_gather(frames_in[0, 0], slot_order(server_of_clip), dp, heads, width)
+    q, k, v = project(residual, ln1_gain[None], ln1_bias[None], w_qkv, qv_bias, block)
+    context = attend_gather(q, k, v, heads, block)
+    attended, normed = output_norm(
+        residual, context, w_out, whole_bias[None], ln2_gain[None], ln2_bias[None], block
+    )
+    layer_out = feed_forward(
+        normed, attended, w_up, fc1_bias[None], w_down, fc2_bias[None], heads, block * 2
+    )
+    return layer_out[None, None]
+
+
+def aligned(mesh, frames_in, qkv_weight, fc1_weight):
+    dp, heads = mesh.shape["dp"], mesh.shape["head"]
+    groups, width = frames_in.shape[2], frames_in.shape[3] // 4
+    frames = groups * 4
+    return (
+        dp % 4 == 0
+        and heads > 1
+        and frames % dp == 0
+        and groups % (frames // dp) == 0
+        and (frames // dp) % 16 == 0
+        and frames % 80 == 0
+        and width % 128 == 0
+        and (qkv_weight.shape[2] // heads) % (2 * HDIM) == 0
+        and (fc1_weight.shape[1] // heads) % (frames // 5 * 2) == 0
+    )
+
+
 def solution(mesh):
     placed = (
         P("dp", "head", None, None),
@@ -162,10 +556,15 @@
         P("head"),
         P(),
     )
-    return jax.shard_map(
-        on_device,
-        mesh=mesh,
-        in_specs=placed,
-        out_specs=P("dp", "head", None, None),
-        check_vma=False,
-    )
+
+    def layer(*args):
+        body = on_device_aligned if aligned(mesh, args[0], args[3], args[9]) else on_device
+        return jax.shard_map(
+            body,
+            mesh=mesh,
+            in_specs=placed,
+            out_specs=P("dp", "head", None, None),
+            check_vma=False,
+        )(*args)
+
+    return layer

time: 612 us -> 354 us (0.58); the launches traced: 602 us -> 354 us
  Pallas kernels: 0 us -> 216 us
  waiting for transfers between devices: 292 us -> 96.2 us
  matrix products: 108 us -> 0 us
  other arithmetic: 57.1 us -> 1.03 us
  blocking collectives: 58.1 us -> 4.36 us
  local copies, waits for them, and re-layouts: 64.6 us -> 22.5 us
  starting transfers between devices: 8.18 us -> 0.12 us
    pallas_call x0 -> x5, Pallas kernels: none -> 216 us  [the longest x1 110 us: regroup_gather(): pl.pallas_call(functools.partial(regroup_kernel, dp, heads), out_shape=ja...]
    dot_general x20 -> x0, matrix products: 108 us -> none  [the longest x1 40.8 us: on_device(): jnp.dot(operand, lax.all_gather(fc1_weight, 'dp', axis=0, tiled=True), pr...]
    reduce_scatter x2 -> x0, waiting for transfers between devices: 88.7 us -> none  [the longest x1 44.9 us: on_device(): lax.psum_scatter(block_term(context, output_rows, frame_count * lax.axis_...]
    all_gather x6 -> x4, waiting for transfers between devices: 164 us -> 94.2 us  [the longest x1 63.7 us: on_device_aligned(): w_down = lax.all_gather(fc2_weight, 'dp', axis=0, tiled=True)]
    all_to_all x1 -> x0, blocking collectives: 58.1 us -> none  [regroup(): lax.all_to_all(picked, 'dp', split_axis=0, concat_axis=0, tiled=True)]
    all_to_all x1 -> x0, waiting for transfers between devices: 36.7 us -> none  [regroup(): lax.all_to_all(piece_rows, 'dp', split_axis=0, concat_axis=0, tiled=True)]
    all_to_all x2 -> x0, other arithmetic: 22.8 us -> none  [the longest x1 11.7 us: regroup(): lax.all_to_all(piece_rows, 'dp', split_axis=0, concat_axis=0, tiled=True)]
    reduce_sum x12 -> x0, other arithmetic: 18.7 us -> none  [the longest x8 7.73 us: single(): jnp.sum(weights, axis=-1, keepdims=True)]
  transfers between devices with their start and end apart: 9 -> 4, of which waited for: 7 -> 2; matrix products, arithmetic and copies ran while one was open for 18% -> 2% of each run, Pallas kernels for 0% -> 47%
where the time goes in v1:
time: 354 us
  Pallas kernels  216 us (61%)
  waiting for transfers between devices  96.2 us (27%)
  local copies, waits for them, and re-layouts  22.5 us (6%)
  between operations  13.2 us (4%)
  blocking collectives  4.36 us (1%)
    pallas_call x1, Pallas kernels, regroup_gather(): pl.pallas_call(functools.partial(regroup_kernel, dp, heads), out_shape=ja...  110 us
    all_gather x1, waiting for transfers between devices, on_device_aligned(): w_down = lax.all_gather(fc2_weight, 'dp', axis=0, tiled=True)  63.7 us
    pallas_call x1, Pallas kernels, feed_forward(): pl.pallas_call(functools.partial(feed_kernel, heads, tile), out_shape=jax...  51.1 us
    pallas_call x1, Pallas kernels, attend_gather(): pl.pallas_call(functools.partial(attend_kernel, heads, block), out_shape=...  40.9 us
    all_gather x1, waiting for transfers between devices, on_device_aligned(): w_up = lax.all_gather(fc1_weight, 'dp', axis=0, tiled=True)  30.5 us
    unnamed x18, local copies, waits for them, and re-layouts  15.5 us
    pallas_call x1, Pallas kernels, project(): pl.pallas_call(project_kernel, grid=(rows // block,), out_shape=[jax.Shap...  7.88 us
  transfers between devices with their start and end apart: 4, of which 2 were waited for; matrix products, arithmetic and copies ran while one was open for 2% of the time, Pallas kernels for 47%

profile of v1, /device:TPU:0, one launch (start us, length us, event | category | flops | bytes accessed | tf_op | source)
XLA Modules:
  0.0 353.6 jit_solution(1048927855976139408)
XLA Ops:
  6.5 0.0 all-gather.6.cloned.1.call-start
  6.5 1.7 copy.19
  8.2 0.0 all-gather.6.cloned.1.call-update
  8.2 0.0 all-gather.8.cloned.1.call-start
  8.3 0.7 all-gather.8.cloned.1.call-update
  9.0 0.0 all-gather.10.cloned.1.call-start
  9.0 0.7 all-gather.10.cloned.1.call-update
  9.7 0.0 copy-start.3
  9.7 0.0 all-gather.12.cloned.1.call-start
  9.8 0.5 all-gather.12.cloned.1.call-update
  10.3 0.7 broadcast_in_dim.44.gain_ref
  11.0 0.7 broadcast_in_dim.45.shift_ref
  11.7 0.7 reshape.7
  12.4 0.7 broadcast_in_dim.47.gain_ref
  13.1 0.7 broadcast_in_dim.48.shift_ref
  13.8 1.3 broadcast_in_dim.49.b1_ref
  15.1 1.3 broadcast_in_dim.50.b2_ref
  16.4 0.9 convert_reduce_fusion
  17.3 0.1 select_reduce_fusion.order_ref
  17.4 0.0 copy-start
  17.4 1.4 copy-done
  18.8 110.0 %regroup.1.x_ref = bf16[1280,1280]{1,0:T(8,128)(2,1)S(1)} custom-call(s32[16]{0:T(128)S(1)} %select_reduce_fusion.order_ref, bf16[320,2560]{1,0:T(8,128)(2,1)S(1)} %bitcast.5), custom_call_target="tpu_custom_call" | custom-call | bytes 200000000 | tf_op jit(solution)/shard_map/regroup/pallas_call | solution.py:248
  128.9 4.4 %all-gather = f32[2,1,640]{2,1,0:T(1,128)S(1)} all-gather(f32[1,1,640]{2,1,0:T(1,128)S(1)} %reshape.7), channel_id=1, replica_groups=mesh['dp'=16,'head'=2] {'head'}, dimensions={0}, use_global_device_ids=true | all-gather | bytes 7680 | tf_op jit(solution)/shard_map/all_gather | solution.py:506
  133.3 0.0 all-gather.6.cloned.1.call-done.w_ref
  133.3 0.0 copy-done.3
  133.3 0.0 copy-start.1
  133.3 2.1 copy-done.1
  135.4 7.9 %project.1 = (bf16[1280,512]{1,0:T(8,128)(2,1)S(1)}, bf16[1280,512]{1,0:T(8,128)(2,1)S(1)}, bf16[1280,512]{1,0:T(8,128)(2,1)S(1)}) custom-call(bf16[1280,1280]{1,0:T(8,128)(2,1)S(1)} %regroup.1.x_ref, f32[1,1280]{1,0:T(1,128)S(1)} %broadcast_in_dim.44.gain_ref, f32[1,1280]{1,0:T(1,128)S(1)} %broadcast_in_dim.45.shift_ref, bf16[1280,1536]{1,0:T(8,128)(2,1)S(1)} %copy-done.1, ...), custom_call_target="tpu_custom_call" | custom-call | flops 5033164800 | bytes 12000000 | tf_op jit(solution)/shard_map/project/pallas_call | solution.py:289
  143.3 40.9 %attend.1.c_ref = bf16[1280,1024]{1,0:T(8,128)(2,1)S(1)} custom-call(bf16[1280,512]{1,0:T(8,128)(2,1)S(1)} %get-tuple-element.10.q_ref, bf16[1280,512]{1,0:T(8,128)(2,1)S(1)} %get-tuple-element.11.k_ref, bf16[1280,512]{1,0:T(8,128)(2,1)S(1)} %get-tuple-element.12.v_ref), custom_call_target="tpu_custom_call" | custom-call | flops 20000000000 | bytes 6000000 | tf_op jit(solution)/shard_map/attend/pallas_call | solution.py:361
  184.2 0.0 copy-start.6
  184.2 1.4 copy-done.6
  185.6 0.0 all-gather.8.cloned.1.call-done.w_ref
  185.6 0.0 copy-start.2
  185.6 1.8 copy-done.2
  187.4 0.0 copy-start.7
  187.4 1.7 copy-done.7
  189.1 6.3 %output.1 = (bf16[1280,1280]{1,0:T(8,128)(2,1)S(1)}, bf16[1280,1280]{1,0:T(8,128)(2,1)S(1)}) custom-call(bf16[1280,1280]{1,0:T(8,128)(2,1)S(1)} %regroup.1.x_ref, bf16[1280,1024]{1,0:T(8,128)(2,1)S(1)} %copy-done.7, bf16[1024,1280]{1,0:T(8,128)(2,1)S(1)} %copy-done.2, f32[1,1280]{1,0:T(1,128)S(1)} %bitcast.6, f32[1,1280]{1,0:T(1,128)S(1)} %broadcast_in_dim.47.gain_ref, ...), custom_call_target="tpu_custom_call" | custom-call | flops 3355443200 | bytes 14000000 | tf_op jit(solution)/shard_map/output/pallas_call | solution.py:388
  195.4 0.0 copy-start.4
  195.4 1.9 copy-done.4
  197.4 0.0 copy-start.5
  197.4 1.7 copy-done.5
  199.0 30.5 %all-gather.10.cloned.1.call-done.w1_ref = bf16[1280,2560]{1,0:T(8,128)(2,1)} async-done(((bf16[80,2560]{1,0:T(8,128)(2,1)}), bf16[1280,2560]{1,0:T(8,128)(2,1)}) %all-gather.10.cloned.1.call-update) | async-done | bytes 6553616 | tf_op jit(solution)/shard_map/all_gather | solution.py:511
  229.5 63.7 %all-gather.12.cloned.1.call-done.w2_ref = bf16[2560,1280]{1,0:T(8,128)(2,1)} async-done(((bf16[160,1280]{1,0:T(8,128)(2,1)}), bf16[2560,1280]{1,0:T(8,128)(2,1)}) %all-gather.12.cloned.1.call-update) | async-done | bytes 6553616 | tf_op jit(solution)/shard_map/all_gather | solution.py:512
  293.3 51.1 %feed.1 = bf16[320,2560]{1,0:T(8,128)(2,1)} custom-call(bf16[1280,1280]{1,0:T(8,128)(2,1)} %copy-done.5, bf16[1280,1280]{1,0:T(8,128)(2,1)} %copy-done.4, bf16[1280,2560]{1,0:T(8,128)(2,1)} %all-gather.10.cloned.1.call-done.w1_ref, f32[1,2560]{1,0:T(1,128)} %broadcast_in_dim.49.b1_ref, bf16[2560,1280]{1,0:T(8,128)(2,1)} %all-gather.12.cloned.1.call-done.w2_ref, ...), custom_call_target="tpu_custom_call" | custom-call | flops 16777216000 | bytes 40000000 | tf_op jit(solution)/shard_map/feed/pallas_call | solution.py:464
  344.4 2.7 copy.21
Async XLA Ops:
  6.5 126.7 %all-gather.6.cloned.1.call-start = ((), (), s32[]{:S(2)}) async-start(), calls=%async_computation | async-start | bytes 4177920 | tf_op jit(solution)/shard_map/all_gather | solution.py:507
  8.2 177.4 %all-gather.8.cloned.1.call-start = ((), (), s32[]{:S(2)}) async-start(), calls=%async_computation.1 | async-start | bytes 2703360 | tf_op jit(solution)/shard_map/all_gather | solution.py:510
  9.0 220.5 %all-gather.10.cloned.1.call-start = ((), (), s32[]{:S(2)}) async-start(), calls=%async_computation.2 | async-start | bytes 6963200 | tf_op jit(solution)/shard_map/all_gather | solution.py:511
  9.7 123.6 %copy-start.3 = (f32[2,512]{1,0:T(2,128)S(1)}, f32[2,512]{1,0:T(2,128)}, u32[]{:S(2)}) copy-start(f32[2,512]{1,0:T(2,128)} %b_ref.1) | copy-start | bytes 12292
  9.7 283.5 %all-gather.12.cloned.1.call-start = ((), (), s32[]{:S(2)}) async-start(), calls=%async_computation.3 | async-start | bytes 6963200 | tf_op jit(solution)/shard_map/all_gather | solution.py:512
  17.4 1.4 copy-start
  133.3 2.1 copy-start.1
  184.2 1.5 copy-start.6
  185.6 1.8 copy-start.2
  187.4 1.8 copy-start.7
  195.4 1.9 copy-start.4
  197.4 1.7 copy-start.5
Sparse Core Ops, SparseCore 0:
  9.6 93.0 all-gather.5
  105.6 60.8 all-gather.7
  168.8 60.6 all-gather.9
  231.6 61.5 all-gather.11

commit v2 on v1

--- a/solution.py
+++ b/solution.py
@@ -300,12 +300,51 @@
     )(x, gain, shift, weight, bias)
 
 
-def attend_kernel(heads, block, q_ref, k_ref, v_ref, o_ref, send, recv):
+def attend_kernel(
+    dp, heads, block, q_ref, k_ref, v_ref, w_ref, o_ref, all_ref, send, recv, ys, yr, ws, wr, own_sem
+):
     me, h = lax.axis_index("dp"), lax.axis_index("head")
     frames, columns = q_ref.shape
     pair = 2 * HDIM
     pairs = columns // pair
-    greet([(me, lax.rem(h + j, heads)) for j in range(1, heads)])
+    greet(
+        [(me, lax.rem(h + j, heads)) for j in range(1, heads)]
+        + [(lax.rem(me + k, dp), h) for k in range(1, dp)]
+    )
+
+    def weight_rows(j):
+        index = lax.rem(h + j, heads) * dp + me
+        return all_ref.at[at_rows(index, w_ref.shape[0])]
+
+    def across(j):
+        return pltpu.make_async_remote_copy(
+            w_ref, weight_rows(0), ys.at[j - 1], yr.at[j - 1], (me, lax.rem(h + j, heads)), MESH
+        )
+
+    def along(k, j):
+        ref = weight_rows(j)
+        return pltpu.make_async_remote_copy(
+            ref, ref, ws.at[j, k], wr.at[j, k], (lax.rem(me + k, dp), h), MESH
+        )
+
+    for j in range(1, heads):
+        across(j).start()
+    mine = pltpu.make_async_copy(w_ref, weight_rows(0), own_sem)
+    mine.start()
+    mine.wait()
+
+    def start_along(j):
+        def step(k, carry):
+            along(k, j).start()
+            return carry
+
+        lax.fori_loop(1, dp, step, 0)
+
+    start_along(0)
+    for j in range(1, heads):
+        across(j).wait()
+    for j in range(1, heads):
+        start_along(j)
     lane = lax.broadcasted_iota(jnp.int32, (1, pair), 1)
     low_f = jnp.where(lane < HDIM, 1.0, 0.0)
     low, high = low_f.astype(jnp.bfloat16), (1.0 - low_f).astype(jnp.bfloat16)
@@ -353,17 +392,30 @@
 
     lax.fori_loop(0, pairs, finish, 0)
 
-
-def attend_gather(q, k, v, heads, block):
+    def finish_along(k, carry):
+        for j in range(heads):
+            along(k, j).wait()
+        return carry
+
+    lax.fori_loop(1, dp, finish_along, 0)
+
+
+def attend_gather(q, k, v, weight, dp, heads, block):
     frames, columns = q.shape
     pairs = columns // (2 * HDIM)
     whole = pl.BlockSpec(memory_space=VMEM)
     return pl.pallas_call(
-        functools.partial(attend_kernel, heads, block),
-        out_shape=jax.ShapeDtypeStruct((frames, heads * columns), q.dtype),
-        in_specs=[whole] * 3,
-        out_specs=whole,
-        scratch_shapes=[pltpu.SemaphoreType.DMA((heads - 1, pairs))] * 2,
+        functools.partial(attend_kernel, dp, heads, block),
+        out_shape=[
+            jax.ShapeDtypeStruct((frames, heads * columns), q.dtype),
+            jax.ShapeDtypeStruct((heads * dp * weight.shape[0], weight.shape[1]), weight.dtype),
+        ],
+        in_specs=[whole] * 4,
+        out_specs=[whole] * 2,
+        scratch_shapes=[pltpu.SemaphoreType.DMA((heads - 1, pairs))] * 2
+        + [pltpu.SemaphoreType.DMA((heads - 1,))] * 2
+        + [pltpu.SemaphoreType.DMA((heads, dp))] * 2
+        + [pltpu.SemaphoreType.DMA],
         compiler_params=pltpu.CompilerParams(
             collective_id=1, has_side_effects=True, vmem_limit_bytes=32000000
         ),
@@ -371,7 +423,7 @@
             flops=20000000000, bytes_accessed=6000000, transcendentals=13000000
         ),
         name="attend",
-    )(q, k, v)
+    )(q, k, v, weight)
 
 
 def output_kernel(x_ref, c_ref, w_ref, bias_ref, gain_ref, shift_ref, a_ref, n_ref):
@@ -507,12 +559,11 @@
     w_qkv = lax.all_gather(
         qkv_weight.reshape(qkv_weight.shape[0], -1), "dp", axis=0, tiled=True
     )
-    w_out = lax.all_gather(out_weight, ("head", "dp"), axis=0, tiled=True)
     w_up = lax.all_gather(fc1_weight, "dp", axis=0, tiled=True)
     w_down = lax.all_gather(fc2_weight, "dp", axis=0, tiled=True)
     residual = regroup_gather(frames_in[0, 0], slot_order(server_of_clip), dp, heads, width)
     q, k, v = project(residual, ln1_gain[None], ln1_bias[None], w_qkv, qv_bias, block)
-    context = attend_gather(q, k, v, heads, block)
+    context, w_out = attend_gather(q, k, v, out_weight, dp, heads, block)
     attended, normed = output_norm(
         residual, context, w_out, whole_bias[None], ln2_gain[None], ln2_bias[None], block
     )
@@ -522,7 +573,7 @@
     return layer_out[None, None]
 
 
-def aligned(mesh, frames_in, qkv_weight, fc1_weight):
+def aligned(mesh, frames_in, qkv_weight, out_weight, fc1_weight):
     dp, heads = mesh.shape["dp"], mesh.shape["head"]
     groups, width = frames_in.shape[2], frames_in.shape[3] // 4
     frames = groups * 4
@@ -534,6 +585,7 @@
         and (frames // dp) % 16 == 0
         and frames % 80 == 0
         and width % 128 == 0
+        and out_weight.shape[0] % (dp * heads * 16) == 0
         and (qkv_weight.shape[2] // heads) % (2 * HDIM) == 0
         and (fc1_weight.shape[1] // heads) % (frames // 5 * 2) == 0
     )
@@ -558,7 +610,7 @@
     )
 
     def layer(*args):
-        body = on_device_aligned if aligned(mesh, args[0], args[3], args[9]) else on_device
+        body = on_device_aligned if aligned(mesh, args[0], args[3], args[5], args[9]) else on_device
         return jax.shard_map(
             body,
             mesh=mesh,

time: 354 us -> 330 us (0.932)
  waiting for transfers between devices: 96.2 us -> 35.3 us
  Pallas kernels: 216 us -> 258 us
  local copies, waits for them, and re-layouts: 22.5 us -> 17.3 us
    pallas_call x1, Pallas kernels: 40.9 us -> 83.9 us  [attend_gather(): pl.pallas_call(functools.partial(attend_kernel, dp, heads, block), out_sh...]
    all_gather x1, waiting for transfers between devices: 30.5 us -> 0.01 us  [on_device_aligned(): w_up = lax.all_gather(fc1_weight, 'dp', axis=0, tiled=True)]
    all_gather x1, waiting for transfers between devices: 63.7 us -> 33.9 us  [on_device_aligned(): w_down = lax.all_gather(fc2_weight, 'dp', axis=0, tiled=True)]
    unnamed x18 -> x14, local copies, waits for them, and re-layouts: 15.5 us -> 10.3 us
  transfers between devices with their start and end apart: 4 -> 3, of which waited for: 2 -> 1; matrix products, arithmetic and copies ran while one was open for 2% -> 2% of each run, Pallas kernels for 47% -> 63%
where the time goes in v2:
time: 330 us
  Pallas kernels  258 us (78%)
  waiting for transfers between devices  35.3 us (11%)
  local copies, waits for them, and re-layouts  17.3 us (5%)
  between operations  13.2 us (4%)
  blocking collectives  4.8 us (1%)
    pallas_call x1, Pallas kernels, regroup_gather(): pl.pallas_call(functools.partial(regroup_kernel, dp, heads), out_shape=ja...  109 us
    pallas_call x1, Pallas kernels, attend_gather(): pl.pallas_call(functools.partial(attend_kernel, dp, heads, block), out_sh...  83.9 us
    pallas_call x1, Pallas kernels, feed_forward(): pl.pallas_call(functools.partial(feed_kernel, heads, tile), out_shape=jax...  51.1 us
    all_gather x1, waiting for transfers between devices, on_device_aligned(): w_down = lax.all_gather(fc2_weight, 'dp', axis=0, tiled=True)  33.9 us
    unnamed x14, local copies, waits for them, and re-layouts  10.3 us
    pallas_call x1, Pallas kernels, project(): pl.pallas_call(project_kernel, grid=(rows // block,), out_shape=[jax.Shap...  7.83 us
  transfers between devices with their start and end apart: 3, of which 1 were waited for; matrix products, arithmetic and copies ran while one was open for 2% of the time, Pallas kernels for 63%

profile of v2, /device:TPU:0, one launch (start us, length us, event | category | flops | bytes accessed | tf_op | source)
XLA Modules:
  0.0 329.6 jit_solution(10368391156039031710)
XLA Ops:
  6.5 0.0 all-gather.5.cloned.1.call-start
  6.5 1.7 copy.19
  8.2 0.0 all-gather.5.cloned.1.call-update
  8.2 0.0 all-gather.7.cloned.1.call-start
  8.3 0.7 all-gather.7.cloned.1.call-update
  9.0 0.0 copy-start.3
  9.0 0.0 all-gather.9.cloned.1.call-start
  9.0 0.7 all-gather.9.cloned.1.call-update
  9.7 0.7 broadcast_in_dim.44.gain_ref
  10.4 0.7 broadcast_in_dim.45.shift_ref
  11.1 0.7 reshape.7
  11.8 0.7 broadcast_in_dim.47.gain_ref
  12.5 0.7 broadcast_in_dim.48.shift_ref
  13.2 1.3 broadcast_in_dim.49.b1_ref
  14.5 1.3 broadcast_in_dim.50.b2_ref
  15.8 0.9 convert_reduce_fusion
  16.7 0.1 select_reduce_fusion.order_ref
  16.8 0.0 copy-start
  16.8 1.4 copy-done
  18.3 108.7 %regroup.1.x_ref = bf16[1280,1280]{1,0:T(8,128)(2,1)S(1)} custom-call(s32[16]{0:T(128)S(1)} %select_reduce_fusion.order_ref, bf16[320,2560]{1,0:T(8,128)(2,1)S(1)} %bitcast.5), custom_call_target="tpu_custom_call" | custom-call | bytes 200000000 | tf_op jit(solution)/shard_map/regroup/pallas_call | solution.py:248
  127.0 4.8 %all-gather = f32[2,1,640]{2,1,0:T(1,128)S(1)} all-gather(f32[1,1,640]{2,1,0:T(1,128)S(1)} %reshape.7), channel_id=1, replica_groups=mesh['dp'=16,'head'=2] {'head'}, dimensions={0}, use_global_device_ids=true | all-gather | bytes 7680 | tf_op jit(solution)/shard_map/all_gather | solution.py:558
  131.8 0.0 all-gather.5.cloned.1.call-done.w_ref
  131.8 0.0 copy-done.3
  131.8 0.0 copy-start.1
  131.8 2.1 copy-done.1
  133.9 0.0 copy-start.2
  133.9 7.8 %project.1 = (bf16[1280,512]{1,0:T(8,128)(2,1)S(1)}, bf16[1280,512]{1,0:T(8,128)(2,1)S(1)}, bf16[1280,512]{1,0:T(8,128)(2,1)S(1)}) custom-call(bf16[1280,1280]{1,0:T(8,128)(2,1)S(1)} %regroup.1.x_ref, f32[1,1280]{1,0:T(1,128)S(1)} %broadcast_in_dim.44.gain_ref, f32[1,1280]{1,0:T(1,128)S(1)} %broadcast_in_dim.45.shift_ref, bf16[1280,1536]{1,0:T(8,128)(2,1)S(1)} %copy-done.1, ...), custom_call_target="tpu_custom_call" | custom-call | flops 5033164800 | bytes 12000000 | tf_op jit(solution)/shard_map/project/pallas_call | solution.py:289
  141.7 0.0 copy-done.2
  141.7 83.9 %attend.1 = (bf16[1280,1024]{1,0:T(8,128)(2,1)S(1)}, bf16[1024,1280]{1,0:T(8,128)(2,1)S(1)}) custom-call(bf16[1280,512]{1,0:T(8,128)(2,1)S(1)} %get-tuple-element.12.q_ref, bf16[1280,512]{1,0:T(8,128)(2,1)S(1)} %get-tuple-element.13.k_ref, bf16[1280,512]{1,0:T(8,128)(2,1)S(1)} %get-tuple-element.14.v_ref, bf16[32,1280]{1,0:T(8,128)(2,1)S(1)} %copy-done.2), custom_call_target="tpu_custom_call" | custom-call | flops 20000000000 | bytes 6000000 | tf_op jit(solution)/shard_map/attend/pallas_call | solution.py:407
  225.7 6.3 %output.1 = (bf16[1280,1280]{1,0:T(8,128)(2,1)S(1)}, bf16[1280,1280]{1,0:T(8,128)(2,1)S(1)}) custom-call(bf16[1280,1280]{1,0:T(8,128)(2,1)S(1)} %regroup.1.x_ref, bf16[1280,1024]{1,0:T(8,128)(2,1)S(1)} %get-tuple-element.15.c_ref, bf16[1024,1280]{1,0:T(8,128)(2,1)S(1)} %get-tuple-element.16.w_ref, f32[1,1280]{1,0:T(1,128)S(1)} %bitcast.6, ...), custom_call_target="tpu_custom_call" | custom-call | flops 3355443200 | bytes 14000000 | tf_op jit(solution)/shard_map/output/pallas_call | solution.py:440
  232.0 0.0 copy-start.4
  232.0 1.7 copy-done.4
  233.7 0.0 copy-start.5
  233.7 1.7 copy-done.5
  235.3 0.0 all-gather.7.cloned.1.call-done.w1_ref
  235.3 33.9 %all-gather.9.cloned.1.call-done.w2_ref = bf16[2560,1280]{1,0:T(8,128)(2,1)} async-done(((bf16[160,1280]{1,0:T(8,128)(2,1)}), bf16[2560,1280]{1,0:T(8,128)(2,1)}) %all-gather.9.cloned.1.call-update) | async-done | bytes 6553616 | tf_op jit(solution)/shard_map/all_gather | solution.py:563
  269.2 51.1 %feed.1 = bf16[320,2560]{1,0:T(8,128)(2,1)} custom-call(bf16[1280,1280]{1,0:T(8,128)(2,1)} %copy-done.5, bf16[1280,1280]{1,0:T(8,128)(2,1)} %copy-done.4, bf16[1280,2560]{1,0:T(8,128)(2,1)} %all-gather.7.cloned.1.call-done.w1_ref, f32[1,2560]{1,0:T(1,128)} %broadcast_in_dim.49.b1_ref, bf16[2560,1280]{1,0:T(8,128)(2,1)} %all-gather.9.cloned.1.call-done.w2_ref, ...), custom_call_target="tpu_custom_call" | custom-call | flops 16777216000 | bytes 40000000 | tf_op jit(solution)/shard_map/feed/pallas_call | solution.py:516
  320.3 2.7 copy.21
Async XLA Ops:
  6.5 125.2 %all-gather.5.cloned.1.call-start = ((), (), s32[]{:S(2)}) async-start(), calls=%async_computation | async-start | bytes 4177920 | tf_op jit(solution)/shard_map/all_gather | solution.py:559
  8.2 227.1 %all-gather.7.cloned.1.call-start = ((), (), s32[]{:S(2)}) async-start(), calls=%async_computation.1 | async-start | bytes 6963200 | tf_op jit(solution)/shard_map/all_gather | solution.py:562
  9.0 122.8 %copy-start.3 = (f32[2,512]{1,0:T(2,128)S(1)}, f32[2,512]{1,0:T(2,128)}, u32[]{:S(2)}) copy-start(f32[2,512]{1,0:T(2,128)} %b_ref.1) | copy-start | bytes 12292
  9.0 260.3 %all-gather.9.cloned.1.call-start = ((), (), s32[]{:S(2)}) async-start(), calls=%async_computation.2 | async-start | bytes 6963200 | tf_op jit(solution)/shard_map/all_gather | solution.py:563
  16.8 1.4 copy-start
  131.8 2.1 copy-start.1
  133.9 7.8 %copy-start.2 = (bf16[32,1280]{1,0:T(8,128)(2,1)S(1)}, bf16[32,1280]{1,0:T(8,128)(2,1)}, u32[]{:S(2)}) copy-start(bf16[32,1280]{1,0:T(8,128)(2,1)} %w_ref.1) | copy-start | bytes 245764
  232.0 1.7 copy-start.4
  233.7 1.7 copy-start.5
Sparse Core Ops, SparseCore 0:
  9.6 92.8 all-gather.4
  104.8 85.4 all-gather.6
  192.7 76.5 all-gather.8
